TPU v7x, 256 devices: a 8x8x2 block of a 8x8x16 slice. The times are simulated.
256 devices in a mesh: groups: 2 (over z), dap: 128 (over x, y, core).
Axes of the slice: x: 8, y: 8, z: 2, core: 2. Of those that a mesh axis runs over, the one named last changes fastest.
The devices are a block of a 8x8x16 slice.
Arguments:
- homolog_tensor: bfloat16 [1024, 256, 256], P(('groups', 'dap')), parts along dimension 0, may hold values from -1 to 1
- couple_tensor: bfloat16 [512, 256, 128], P(('groups', 'dap')), parts along dimension 0, may hold values from -6 to 6
- horizontal_drop_filter: int32 [512, 256], P('groups'), parts along dimension 0, may hold values 0 or 1
- couple_offset_matrix: bfloat16 [128, 8], replicated, may hold values from -0.29882812 to 0.29882812
- horizontal_attend_matrix: bfloat16 [256, 1024], replicated, may hold values from -0.375 to 0.375
- horizontal_exit_matrix: bfloat16 [256, 256], replicated, may hold values from -0.375 to 0.375
- vertical_attend_matrix: bfloat16 [256, 1024], replicated, may hold values from -0.375 to 0.375
- vertical_exit_matrix: bfloat16 [256, 256], replicated, may hold values from -0.375 to 0.375
- averaged_product_flanks: bfloat16 [256, 64], replicated, may hold values from -0.375 to 0.375
- averaged_product_exit: bfloat16 [1024, 128], replicated, may hold values from -1 to 1
Outputs:
- alignment_output: bfloat16 [1024, 256, 256], P('groups', 'dap'), parts along dimension 0
- pair_output_state: bfloat16 [512, 256, 128], P(('groups', 'dap')), parts along dimension 0
There are 2 independent parts, one for each index of `groups`. A program takes and returns all parts, laid end to end along the dimension named above; an argument that names none is the same for every part. Nothing has to cross between parts.
All inputs are finite; a program needn't handle non-finite values.
Results may differ from a plain program's by a relative error of at most 0.012.
Values may be sent and summed in bfloat16 or wider, within the bound.
A program may use at most 64 MiB of HBM per device.

v0:
```python
import jax
import jax.numpy as jnp
from jax import lax
from jax.sharding import Mesh
from jax.sharding import PartitionSpec as P

HEAD_NUMBER = 8
HEAD_WIDTH = 32
FACTOR_FEATURES = 32
DAP = ("dap_0", "dap_1", "dap_2")
GROUPS_DAP = ("groups", "dap_0", "dap_1", "dap_2")


def joined_along(tiles, dim):
    tiles = jnp.moveaxis(tiles, 0, dim)
    dims = tiles.shape
    return tiles.reshape(*dims[:dim], dims[dim] * dims[dim + 1], *dims[dim + 2 :])


def stacked_from(shard, axes, order):
    tiles = shard[None]
    for k in order:
        tiles = lax.all_gather(tiles, axes[k], axis=0, tiled=True)
    carried = [lax.axis_size(axes[k]) for k in reversed(order)]
    tiles = tiles.reshape(*carried, *shard.shape)
    turned = sorted(range(len(order)), key=lambda place: order[len(order) - 1 - place])
    return tiles.transpose(*turned, *range(len(order), tiles.ndim)).reshape(-1, *shard.shape)


def gather_axes(shard, axes, order, dim):
    return joined_along(stacked_from(shard, axes, order), dim)


def standardise_features(values):
    values = values.astype(jnp.float32)
    center = values - jnp.mean(values, axis=-1, keepdims=True)
    spread = jnp.mean(center * center, axis=-1, keepdims=True)
    return center * lax.rsqrt(spread + 1e-05)


def attend(normed, w_qkvg, w_out, bias):
    batch, length = (normed.shape[0], normed.shape[1])
    proj = jnp.einsum("blc,cf->blf", normed, w_qkvg, preferred_element_type=jnp.float32)
    proj = proj.reshape(batch, length, 4, HEAD_NUMBER, HEAD_WIDTH)
    query = (proj[:, :, 0] * HEAD_WIDTH ** (-0.5)).astype(jnp.bfloat16)
    keys = proj[:, :, 1].astype(jnp.bfloat16)
    values = proj[:, :, 2].astype(jnp.bfloat16)
    gate = proj[:, :, 3]
    if bias is None:
        bias = jnp.zeros((HEAD_NUMBER, length, length), jnp.bfloat16)

    def one_head(items):
        qh, kh, vh, bh = items
        scores = jnp.einsum("bid,bjd->bij", qh, kh, preferred_element_type=jnp.float32)
        scores = scores + bh.astype(jnp.float32)[None]
        weights = jax.nn.softmax(scores, axis=-1).astype(jnp.bfloat16)
        return jnp.einsum("bij,bjd->bid", weights, vh, preferred_element_type=jnp.float32)

    heads = lax.map(
        one_head,
        (jnp.moveaxis(query, 2, 0), jnp.moveaxis(keys, 2, 0), jnp.moveaxis(values, 2, 0), bias),
    )
    heads = jnp.moveaxis(heads, 0, 2)
    gated = (
        (jax.nn.sigmoid(gate) * heads)
        .astype(jnp.bfloat16)
        .reshape(batch, length, HEAD_NUMBER * HEAD_WIDTH)
    )
    return jnp.einsum("blk,kc->blc", gated, w_out, preferred_element_type=jnp.float32)


def shards(
    homolog_tensor,
    couple_tensor,
    horizontal_drop_filter,
    couple_offset_matrix,
    horizontal_attend_matrix,
    horizontal_exit_matrix,
    vertical_attend_matrix,
    vertical_exit_matrix,
    averaged_product_flanks,
    averaged_product_exit,
):
    normed_pair = standardise_features(couple_tensor).astype(jnp.bfloat16)
    own_bias = jnp.einsum(
        "ijz,zh->hij", normed_pair, couple_offset_matrix, preferred_element_type=jnp.float32
    ).astype(jnp.bfloat16)
    bias = gather_axes(own_bias, DAP, (0, 1, 2), 1)
    starting_answer = standardise_features(homolog_tensor).astype(jnp.bfloat16)
    perform_refresh = attend(
        starting_answer, horizontal_attend_matrix, horizontal_exit_matrix, bias
    )
    homolog_later = (
        homolog_tensor.astype(jnp.float32)
        + horizontal_drop_filter.astype(jnp.float32) * (1.0 / 0.9) * perform_refresh
    ).astype(jnp.bfloat16)
    incoming_blocks = lax.all_to_all(homolog_later, DAP, split_axis=1, concat_axis=0, tiled=True)
    column_layout = jnp.swapaxes(incoming_blocks, 0, 1)
    perform_refresh = attend(
        standardise_features(column_layout).astype(jnp.bfloat16),
        vertical_attend_matrix,
        vertical_exit_matrix,
        None,
    )
    alignment_output = jnp.swapaxes(
        (column_layout.astype(jnp.float32) + perform_refresh).astype(jnp.bfloat16), 0, 1
    )
    final_result = standardise_features(alignment_output).astype(jnp.bfloat16)
    factors = jnp.einsum(
        "sic,cf->sif", final_result, averaged_product_flanks, preferred_element_type=jnp.float32
    )
    left = factors[..., :FACTOR_FEATURES].astype(jnp.bfloat16)
    right = factors[..., FACTOR_FEATURES:].astype(jnp.bfloat16)
    total = left.shape[0]
    own_rows = left.shape[1]
    piece = lax.all_gather(right, DAP, axis=1, tiled=True)
    outer = jnp.einsum("sic,sjd->ijcd", left, piece, preferred_element_type=jnp.float32) / total
    outer = outer.astype(jnp.bfloat16).reshape(
        own_rows, piece.shape[1], FACTOR_FEATURES * FACTOR_FEATURES
    )
    change = jnp.einsum(
        "ijk,kz->ijz", outer, averaged_product_exit, preferred_element_type=jnp.float32
    )
    pair_output_state = (couple_tensor.astype(jnp.float32) + change).astype(jnp.bfloat16)
    return (alignment_output, pair_output_state)


def solution(mesh):
    torus = Mesh(
        mesh.devices.reshape(mesh.shape["groups"], 8, 8, 2), ("groups", "dap_0", "dap_1", "dap_2")
    )
    return jax.shard_map(
        shards,
        mesh=torus,
        in_specs=(
            P(GROUPS_DAP, None, None),
            P(GROUPS_DAP, None, None),
            P("groups", None),
            P(),
            P(),
            P(),
            P(),
            P(),
            P(),
            P(),
        ),
        out_specs=(P("groups", DAP, None), P(GROUPS_DAP, None, None)),
        check_vma=False,
    )
```

profile of v0, /device:TPU:513, one launch (start us, length us, event | category | flops | bytes accessed | tf_op | source)
XLA Modules:
  0.0 365.0 jit_solution(12928804633516290471)
XLA Ops:
  9.5 1.2 fusion.37
  10.7 20.9 %all-gather = bf16[64,2,256]{2,0,1:T(8,128)(2,1)S(1)} all-gather(bf16[8,2,256]{2,0,1:T(8,128)(2,1)S(1)} %fusion.37), channel_id=2, replica_groups=mesh['groups'=2,'dap_0'=8,'dap_1'=8,'dap_2'=2] {'dap_0'}, dimensions={0}, use_global_device_ids=true | all-gather | bytes 73728 | tf_op jit(solution)/shard_map/all_gather | solution.py:23
  31.7 30.9 %all_gather.13 = bf16[64,8,2,256]{3,1,0,2:T(8,128)(2,1)} all-gather(bf16[8,8,2,256]{3,1,0,2:T(8,128)(2,1)S(1)} %bitcast.194), channel_id=1, replica_groups=mesh['groups'=2,'dap_0'=8,'dap_1'=8,'dap_2'=2] {'dap_1'}, dimensions={0}, use_global_device_ids=true | all-gather | bytes 589824 | tf_op jit(solution)/shard_map/all_gather | solution.py:23
  62.6 1.3 convert_reduce_fusion
  63.9 1.4 fusion.38
  65.3 2.0 fusion.59
  71.5 27.3 %all-gather.4.cloned.1.call-done = bf16[128,8,2,256]{3,1,0,2:T(8,128)(2,1)} async-done(((bf16[64,8,2,256]{3,1,0,2:T(8,128)(2,1)}), bf16[128,8,2,256]{3,1,0,2:T(8,128)(2,1)}) %all-gather.4.cloned.1.call-update) | async-done | bytes 1048592 | tf_op jit(solution)/shard_map/all_gather | solution.py:23
  98.8 1.4 copy.52
  101.0 36.0 %while.20 = (s32[]{:T(128)}, f32[8,4,256,32]{2,3,0,1:T(8,128)}, bf16[8,4,256,32]{2,3,0,1:T(8,128)(2,1)}, bf16[8,4,256,32]{2,3,0,1:T(8,128)(2,1)}, bf16[8,256,256...) while((s32[]{:T(128)}, f32[8,4,256,32]{2,3,0,1:T(8,128)}, ...), condition=%wide.region_7.8_spmd, body=%wide.region_4.7_spmd.sunk | while | flops 52233728 | bytes 4533337 | solution.py:59
  101.0 1.4 fusion.104
  102.4 1.2 convolution_add_fusion.3
  103.7 1.9 fusion.105
  105.6 1.4 fusion.104
  108.2 1.9 fusion.105
  110.0 1.4 fusion.104
  112.6 1.9 fusion.105
  114.5 1.4 fusion.104
  117.1 1.8 fusion.105
  119.0 1.4 fusion.104
  121.6 1.8 fusion.105
  123.5 1.4 fusion.104
  126.1 1.8 fusion.105
  128.0 1.4 fusion.104
  130.6 1.8 fusion.105
  132.4 1.4 fusion.104
  135.1 1.9 fusion.105
  136.9 1.8 fusion.54
  138.8 1.3 fusion.31
  141.3 14.5 %all-to-all-start = ((bf16[4,256,256]{2,0,1:T(4,128)(2,1)}), bf16[4,256,256]{2,0,1:T(4,128)(2,1)S(1)}, u32[]{:S(2)}, u32[]{:S(2)}) async-start(bf16[4,256,256]{2,0,1:T(4,128)(2,1)} %copy.59), calls=%async_computation | async-start | bytes 1048576 | tf_op jit(solution)/shard_map/all_to_all | solution.py:97
  156.1 18.9 %all-to-all-done = bf16[4,256,256]{2,0,1:T(4,128)(2,1)S(1)} async-done(((bf16[4,256,256]{2,0,1:T(4,128)(2,1)}), bf16[4,256,256]{2,0,1:T(4,128)(2,1)S(1)}, u32[]{:S(2)}, u32[]{:S(2)}) %all-to-all-start) | async-done | bytes 524320 | tf_op jit(solution)/shard_map/all_to_all | solution.py:97
  176.0 1.6 multiply_reduce_fusion
  177.6 1.8 multiply_convert_fusion.1
  180.3 1.8 copy-done.1
  182.1 1.7 convert.21
  184.5 2.1 slice_bitcast_fusion
  186.6 73.0 %while.21 = (s32[]{:T(128)}, f32[8,2,512,32]{2,3,0,1:T(8,128)}, bf16[8,2,512,32]{2,3,0,1:T(8,128)(2,1)S(1)}, bf16[8,2,512,32]{2,3,0,1:T(8,128)(2,1)}, bf16[8,2,512,32]{2,3,0,1:T(8,128)(2,1)S(1)}, /*index=5*/s32[]{:T(128)}) while((s32[]{:T(128)}, f32[8,2,512,32]{2,3,0,1:T(8,128)}, bf16[8,2,512,32]{2,3,0,1:T(8,128)(2,1)S(1)}, ...), condition=%wide.region_13.14_spmd, body=%wide.region_10.13_spmd.sunk | while | flops 67108864 | bytes 1507417 | solution.py:59
  190.1 3.8 %dot_general.47 = f32[2,512,32]{2,1,0:T(8,128)} custom-call(bf16[2,512,32]{2,1,0:T(8,128)(2,1)} %bitcast.177, bf16[2,512,32]{2,1,0:T(8,128)(2,1)} %bitcast.176, bf16[2,512,32]{2,1,0:T(8,128)(2,1)} %bitcast.178), custom_call_target="tpu_custom_call" | custom-call | flops 67108864 | bytes 196608 | tf_op jit(solution)/shard_map/while/body/eval_jaxpr/bij,bjd->bid/dot_general | solution.py:57
  199.2 3.8 %dot_general.47 = f32[2,512,32]{2,1,0:T(8,128)} custom-call(bf16[2,512,32]{2,1,0:T(8,128)(2,1)} %bitcast.177, bf16[2,512,32]{2,1,0:T(8,128)(2,1)} %bitcast.176, bf16[2,512,32]{2,1,0:T(8,128)(2,1)} %bitcast.178), custom_call_target="tpu_custom_call" | custom-call | flops 67108864 | bytes 196608 | tf_op jit(solution)/shard_map/while/body/eval_jaxpr/bij,bjd->bid/dot_general | solution.py:57
  208.3 3.8 %dot_general.47 = f32[2,512,32]{2,1,0:T(8,128)} custom-call(bf16[2,512,32]{2,1,0:T(8,128)(2,1)} %bitcast.177, bf16[2,512,32]{2,1,0:T(8,128)(2,1)} %bitcast.176, bf16[2,512,32]{2,1,0:T(8,128)(2,1)} %bitcast.178), custom_call_target="tpu_custom_call" | custom-call | flops 67108864 | bytes 196608 | tf_op jit(solution)/shard_map/while/body/eval_jaxpr/bij,bjd->bid/dot_general | solution.py:57
  217.4 3.8 %dot_general.47 = f32[2,512,32]{2,1,0:T(8,128)} custom-call(bf16[2,512,32]{2,1,0:T(8,128)(2,1)} %bitcast.177, bf16[2,512,32]{2,1,0:T(8,128)(2,1)} %bitcast.176, bf16[2,512,32]{2,1,0:T(8,128)(2,1)} %bitcast.178), custom_call_target="tpu_custom_call" | custom-call | flops 67108864 | bytes 196608 | tf_op jit(solution)/shard_map/while/body/eval_jaxpr/bij,bjd->bid/dot_general | solution.py:57
  226.6 3.8 %dot_general.47 = f32[2,512,32]{2,1,0:T(8,128)} custom-call(bf16[2,512,32]{2,1,0:T(8,128)(2,1)} %bitcast.177, bf16[2,512,32]{2,1,0:T(8,128)(2,1)} %bitcast.176, bf16[2,512,32]{2,1,0:T(8,128)(2,1)} %bitcast.178), custom_call_target="tpu_custom_call" | custom-call | flops 67108864 | bytes 196608 | tf_op jit(solution)/shard_map/while/body/eval_jaxpr/bij,bjd->bid/dot_general | solution.py:57
  235.7 3.8 %dot_general.47 = f32[2,512,32]{2,1,0:T(8,128)} custom-call(bf16[2,512,32]{2,1,0:T(8,128)(2,1)} %bitcast.177, bf16[2,512,32]{2,1,0:T(8,128)(2,1)} %bitcast.176, bf16[2,512,32]{2,1,0:T(8,128)(2,1)} %bitcast.178), custom_call_target="tpu_custom_call" | custom-call | flops 67108864 | bytes 196608 | tf_op jit(solution)/shard_map/while/body/eval_jaxpr/bij,bjd->bid/dot_general | solution.py:57
  244.8 3.8 %dot_general.47 = f32[2,512,32]{2,1,0:T(8,128)} custom-call(bf16[2,512,32]{2,1,0:T(8,128)(2,1)} %bitcast.177, bf16[2,512,32]{2,1,0:T(8,128)(2,1)} %bitcast.176, bf16[2,512,32]{2,1,0:T(8,128)(2,1)} %bitcast.178), custom_call_target="tpu_custom_call" | custom-call | flops 67108864 | bytes 196608 | tf_op jit(solution)/shard_map/while/body/eval_jaxpr/bij,bjd->bid/dot_general | solution.py:57
  253.9 3.8 %dot_general.47 = f32[2,512,32]{2,1,0:T(8,128)} custom-call(bf16[2,512,32]{2,1,0:T(8,128)(2,1)} %bitcast.177, bf16[2,512,32]{2,1,0:T(8,128)(2,1)} %bitcast.176, bf16[2,512,32]{2,1,0:T(8,128)(2,1)} %bitcast.178), custom_call_target="tpu_custom_call" | custom-call | flops 67108864 | bytes 196608 | tf_op jit(solution)/shard_map/while/body/eval_jaxpr/bij,bjd->bid/dot_general | solution.py:57
  259.7 1.8 fusion.55
  264.1 77.3 %all-gather.6.cloned.1.call-done = bf16[512,256,32]{0,2,1:T(8,128)(2,1)} async-done(((bf16[512,2,32]{0,2,1:T(8,128)(2,1)}), bf16[512,256,32]{0,2,1:T(8,128)(2,1)}) %all-gather.6.cloned.1.call-update) | async-done | bytes 8388624 | tf_op jit(solution)/shard_map/all_gather | solution.py:116
  341.4 9.4 %fusion.26 = bf16[2,256,32,32]{2,3,0,1:T(8,128)(2,1)} fusion(bf16[512,256,32]{0,2,1:T(8,128)(2,1)} %all-gather.6.cloned.1.call-done, bf16[512,2,64]{0,2,1:T(8,128)(2,1)S(1)} %convolution_convert_fusion), kind=kOutput, calls=%fused_computation.30 | convolution fusion | flops 537919488 | bytes 9502720 | tf_op jit(solution)/shard_map/sic,sjd->ijcd/dot_general | solution.py:117
  350.8 6.2 %copy.71 = bf16[2,256,32,32]{1,3,2,0:T(8,128)(2,1)S(1)} copy(bf16[2,256,32,32]{2,3,0,1:T(8,128)(2,1)} %fusion.26) | data formatting | bytes 2097152 | tf_op jit(solution)/shard_map/convert_element_type | solution.py:118
  (125 shorter events, 66.2 us)
Async XLA Ops:
  7.2 58.2 %copy-start = (bf16[256,1024]{1,0:T(8,128)(2,1)S(1)}, bf16[256,1024]{1,0:T(8,128)(2,1)}, u32[]{:S(2)}) copy-start(bf16[256,1024]{1,0:T(8,128)(2,1)} %param.18) | copy-start | bytes 1572868
  7.2 91.6 %all-gather.4.cloned.1.call-start = ((), (), s32[]{:S(2)}) async-start(), calls=%async_computation.1 | async-start | bytes 1572864 | tf_op jit(solution)/shard_map/all_gather | solution.py:23
  67.4 3.0 copy-start.2
  67.4 1.1 copy-start.6
  100.9 37.8 %copy-start.3 = (bf16[4,256,256]{2,1,0:T(8,128)(2,1)S(1)}, bf16[4,256,256]{2,1,0:T(8,128)(2,1)}, u32[]{:S(2)}) copy-start(bf16[4,256,256]{2,1,0:T(8,128)(2,1)} %param.14) | copy-start | bytes 1572868
  101.0 37.8 %copy-start.9 = (bf16[256,256]{1,0:T(8,128)(2,1)S(1)}, bf16[256,256]{1,0:T(8,128)(2,1)}, u32[]{:S(2)}) copy-start(bf16[256,256]{1,0:T(8,128)(2,1)} %param.19) | copy-start | bytes 393220
  141.3 38.1 %copy-start.5 = (bf16[256,1024]{1,0:T(8,128)(2,1)S(1)}, bf16[256,1024]{1,0:T(8,128)(2,1)}, u32[]{:S(2)}) copy-start(bf16[256,1024]{1,0:T(8,128)(2,1)} %param.20) | copy-start | bytes 1572868
  141.3 33.6 %all-to-all-start = ((bf16[4,256,256]{2,0,1:T(4,128)(2,1)}), bf16[4,256,256]{2,0,1:T(4,128)(2,1)S(1)}, u32[]{:S(2)}, u32[]{:S(2)}) async-start(bf16[4,256,256]{2,0,1:T(4,128)(2,1)} %copy.59), calls=%async_computation | async-start | bytes 1048576 | tf_op jit(solution)/shard_map/all_to_all | solution.py:97
  155.8 185.6 %all-gather.6.cloned.1.call-start = ((), (), s32[]{:S(2)}) async-start(), calls=%async_computation.2 | async-start | bytes 8454144 | tf_op jit(solution)/shard_map/all_gather | solution.py:116
  180.1 1.9 copy-start.1
  186.6 74.9 %copy-start.8 = (bf16[256,256]{1,0:T(8,128)(2,1)S(1)}, bf16[256,256]{1,0:T(8,128)(2,1)}, u32[]{:S(2)}) copy-start(bf16[256,256]{1,0:T(8,128)(2,1)} %param.21) | copy-start | bytes 393220
  259.7 2.4 copy-start.10
  350.8 6.2 %copy-start.4 = (bf16[2,256,128]{2,1,0:T(8,128)(2,1)S(1)}, bf16[2,256,128]{2,1,0:T(8,128)(2,1)}, u32[]{:S(2)}) copy-start(bf16[2,256,128]{2,1,0:T(8,128)(2,1)} %param.15) | copy-start | bytes 393220
  350.8 6.2 %copy-start.7 = (bf16[1024,128]{1,0:T(8,128)(2,1)S(1)}, bf16[1024,128]{1,0:T(8,128)(2,1)}, u32[]{:S(2)}) copy-start(bf16[1024,128]{1,0:T(8,128)(2,1)} %param.23) | copy-start | bytes 786436
Sparse Core Ops, SparseCore 0:
  62.7 36.0 all-gather.3
  263.1 78.1 all-gather.5
where the time goes:
time: 368 us; the launch traced here: 365 us
  waiting for transfers between devices  124 us (34%)
  local copies, waits for them, and re-layouts  60.6 us (16%)
  matrix products  52.1 us (14%)
  blocking collectives  51.8 us (14%)
  Pallas kernels  30.7 us (8%)
  other arithmetic  16.8 us (5%)
  starting transfers between devices  14.8 us (4%)
  between operations  14.4 us (4%)
    all_gather x1, waiting for transfers between devices, shards(): piece = lax.all_gather(right, DAP, axis=1, tiled=True)  77.3 us
    all_gather x2, blocking collectives, stacked_from(): tiles = lax.all_gather(tiles, axes[k], axis=0, tiled=True)  51.8 us
    dot_general x8, Pallas kernels, one_head(): jnp.einsum('bij,bjd->bid', weights, vh, preferred_element_type=jnp.float32)  30.7 us
    all_gather x1, waiting for transfers between devices, stacked_from(): tiles = lax.all_gather(tiles, axes[k], axis=0, tiled=True)  27.3 us
    dynamic_slice x40, local copies, waits for them, and re-layouts, attend(): lax.map(one_head, (jnp.moveaxis(query, 2, 0), jnp.moveaxis(keys, 2, 0), j...  27.3 us
    all_to_all x1, waiting for transfers between devices, shards(): lax.all_to_all(homolog_later, DAP, split_axis=1, concat_axis=0, tiled=True)  18.9 us
    dynamic_update_slice x16, local copies, waits for them, and re-layouts, attend(): lax.map(one_head, (jnp.moveaxis(query, 2, 0), jnp.moveaxis(keys, 2, 0), j...  15 us
    dot_general x8, matrix products, one_head(): jnp.einsum('bij,bjd->bid', weights, vh, preferred_element_type=jnp.float32)  14.8 us
  transfers between devices with their start and end apart: 3, of which 3 were waited for; matrix products, arithmetic and copies ran while one was open for 2% of the time, Pallas kernels for 0%

commit v1 on v0

--- a/solution.py
+++ b/solution.py
@@ -20,7 +20,9 @@
 def stacked_from(shard, axes, order):
     tiles = shard[None]
     for k in order:
-        tiles = lax.all_gather(tiles, axes[k], axis=0, tiled=True)
+        tiles = jnp.concatenate(
+            lax.all_to_all(jnp.stack([tiles] * lax.axis_size(axes[k])), axes[k], 0, 0), axis=0
+        )
     carried = [lax.axis_size(axes[k]) for k in reversed(order)]
     tiles = tiles.reshape(*carried, *shard.shape)
     turned = sorted(range(len(order)), key=lambda place: order[len(order) - 1 - place])

time: 368 us -> 334 us (0.908)
  blocking collectives: 51.8 us -> 12.1 us
  starting transfers between devices: 14.8 us -> 29.9 us
  waiting for transfers between devices: 124 us -> 110 us
    all_gather x2 -> x0, blocking collectives: 51.8 us -> none  [stacked_from(): tiles = lax.all_gather(tiles, axes[k], axis=0, tiled=True)]
    all_gather x1 -> x0, waiting for transfers between devices: 27.3 us -> none  [stacked_from(): tiles = lax.all_gather(tiles, axes[k], axis=0, tiled=True)]
    all_to_all x0 -> x2, starting transfers between devices: none -> 20.8 us  [stacked_from(): lax.all_to_all(jnp.stack([tiles] * lax.axis_size(axes[k])), axes[k], 0, 0)]
    all_to_all x0 -> x1, blocking collectives: none -> 12.1 us  [stacked_from(): lax.all_to_all(jnp.stack([tiles] * lax.axis_size(axes[k])), axes[k], 0, 0)]
    all_gather x1, waiting for transfers between devices: 77.3 us -> 84.4 us  [shards(): piece = lax.all_gather(right, DAP, axis=1, tiled=True)]
    all_to_all x0 -> x2, waiting for transfers between devices: none -> 6.24 us  [stacked_from(): lax.all_to_all(jnp.stack([tiles] * lax.axis_size(axes[k])), axes[k], 0, 0)]
    all_to_all x1, starting transfers between devices: 14.5 us -> 8.88 us  [shards(): lax.all_to_all(homolog_later, DAP, split_axis=1, concat_axis=0, tiled=True)]
  transfers between devices with their start and end apart: 3 -> 4, of which waited for: 3 -> 4; matrix products, arithmetic and copies ran while one was open for 2% -> 4% of each run, Pallas kernels for 0% -> 0%
where the time goes in v1:
time: 334 us; the launch traced here: 331 us
  waiting for transfers between devices  110 us (33%)
  local copies, waits for them, and re-layouts  60.1 us (18%)
  matrix products  54.1 us (16%)
  Pallas kernels  30.7 us (9%)
  starting transfers between devices  29.9 us (9%)
  other arithmetic  20.2 us (6%)
  between operations  14.4 us (4%)
  blocking collectives  12.1 us (4%)
    all_gather x1, waiting for transfers between devices, shards(): piece = lax.all_gather(right, DAP, axis=1, tiled=True)  84.4 us
    dot_general x8, Pallas kernels, one_head(): jnp.einsum('bij,bjd->bid', weights, vh, preferred_element_type=jnp.float32)  30.7 us
    dynamic_slice x40, local copies, waits for them, and re-layouts, attend(): lax.map(one_head, (jnp.moveaxis(query, 2, 0), jnp.moveaxis(keys, 2, 0), j...  27.3 us
    all_to_all x2, starting transfers between devices, stacked_from(): lax.all_to_all(jnp.stack([tiles] * lax.axis_size(axes[k])), axes[k], 0, 0)  20.8 us
    all_to_all x1, waiting for transfers between devices, shards(): lax.all_to_all(homolog_later, DAP, split_axis=1, concat_axis=0, tiled=True)  18.9 us
    dynamic_update_slice x16, local copies, waits for them, and re-layouts, attend(): lax.map(one_head, (jnp.moveaxis(query, 2, 0), jnp.moveaxis(keys, 2, 0), j...  15 us
    dot_general x8, matrix products, one_head(): jnp.einsum('bij,bjd->bid', weights, vh, preferred_element_type=jnp.float32)  14.8 us
    all_to_all x1, blocking collectives, stacked_from(): lax.all_to_all(jnp.stack([tiles] * lax.axis_size(axes[k])), axes[k], 0, 0)  12.1 us
  transfers between devices with their start and end apart: 4, of which 4 were waited for; matrix products, arithmetic and copies ran while one was open for 4% of the time, Pallas kernels for 0%

profile of v1, /device:TPU:513, one launch (start us, length us, event | category | flops | bytes accessed | tf_op | source)
XLA Modules:
  0.0 331.2 jit_solution(6684515352287282470)
XLA Ops:
  11.3 7.9 %all-to-all-start = ((bf16[8,1,8,2,256]{4,2,3,1,0:T(8,128)(2,1)}), bf16[8,1,8,2,256]{4,2,3,1,0:T(8,128)(2,1)S(1)}, u32[]{:S(2)}, u32[]{:S(2)}) async-start(bf16[8,1,8,2,256]{4,2,3,1,0:T(8,128)(2,1)} %stack.9), calls=%async_computation | async-start | bytes 131072 | tf_op jit(solution)/shard_map/all_to_all | solution.py:24
  20.4 1.4 fusion.38
  21.9 4.5 %all-to-all-done = bf16[8,1,8,2,256]{4,2,3,1,0:T(8,128)(2,1)S(1)} async-done(((bf16[8,1,8,2,256]{4,2,3,1,0:T(8,128)(2,1)}), bf16[8,1,8,2,256]{4,2,3,1,0:T(8,128)(2,1)S(1)}, u32[]{:S(2)}, u32[]{:S(2)}) %all-to-all-start) | async-done | bytes 65568 | tf_op jit(solution)/shard_map/all_to_all | solution.py:24
  27.2 13.0 %all-to-all-start.1 = ((bf16[8,8,8,2,256]{4,2,3,1,0:T(8,128)(2,1)}), bf16[8,8,8,2,256]{4,2,3,1,0:T(8,128)(2,1)S(1)}, u32[]{:S(2)}, u32[]{:S(2)}) async-start(bf16[8,8,8,2,256]{4,2,3,1,0:T(8,128)(2,1)} %stack.10), calls=%async_computation.1 | async-start | bytes 1048576 | tf_op jit(solution)/shard_map/all_to_all | solution.py:24
  40.2 3.9 %fusion.59 = f32[4,256,1024]{1,2,0:T(8,128)} fusion(bf16[4,256,256]{2,1,0:T(8,128)(2,1)} %param.14, bf16[256,1024]{1,0:T(8,128)(2,1)S(1)} %copy-done, f32[4,256]{1,0:T(4,128)S(1)} %add_rsqrt_fusion.2, f32[4,256]{1,0:T(4,128)S(1)} %broadcast_multiply_fusion.2), kind=kOutput, calls=%fused_computation.77 | convolution fusion | flops 537919488 | bytes 5251072 | tf_op jit(solution)/shard_map/blc,cf->blf/dot_general | solution.py:45
  44.2 2.6 convert.20
  47.5 2.1 fusion.56
  50.7 1.7 all-to-all-done.1
  52.6 12.1 %all_to_all.24 = bf16[2,64,8,2,256]{4,2,3,1,0:T(8,128)(2,1)S(1)} all-to-all(bf16[2,64,8,2,256]{4,2,3,1,0:T(8,128)(2,1)S(1)} %pad_maximum_fusion), channel_id=1, replica_groups=mesh['groups'=2,'dap_0'=8,'dap_1'=8,'dap_2'=2] {'dap_2'}, dimensions={0} | all-to-all | bytes 2097152 | tf_op jit(solution)/shard_map/all_to_all | solution.py:24
  65.6 36.0 %while.20 = (s32[]{:T(128)}, f32[8,4,256,32]{2,3,0,1:T(8,128)}, bf16[8,4,256,32]{2,3,0,1:T(8,128)(2,1)}, bf16[8,4,256,32]{2,3,0,1:T(8,128)(2,1)}, bf16[8,256,256...) while((s32[]{:T(128)}, f32[8,4,256,32]{2,3,0,1:T(8,128)}, ...), condition=%wide.region_7.8_spmd, body=%wide.region_4.7_spmd.sunk | while | flops 52233728 | bytes 4533337 | solution.py:61
  65.6 1.4 fusion.104
  68.3 1.9 fusion.105
  70.2 1.4 fusion.104
  72.8 1.9 fusion.105
  74.7 1.4 fusion.104
  77.3 1.9 fusion.105
  79.2 1.4 fusion.104
  81.8 1.8 fusion.105
  83.6 1.4 fusion.104
  86.2 1.8 fusion.105
  88.1 1.4 fusion.104
  90.7 1.8 fusion.105
  92.6 1.4 fusion.104
  95.2 1.8 fusion.105
  97.1 1.4 fusion.104
  99.7 1.9 fusion.105
  101.6 1.8 fusion.54
  103.4 1.3 fusion.31
  105.9 8.9 %all-to-all-start.3 = ((bf16[4,256,256]{2,0,1:T(4,128)(2,1)}), bf16[4,256,256]{2,0,1:T(4,128)(2,1)S(1)}, u32[]{:S(2)}, u32[]{:S(2)}) async-start(bf16[4,256,256]{2,0,1:T(4,128)(2,1)} %copy.81), calls=%async_computation.3 | async-start | bytes 1048576 | tf_op jit(solution)/shard_map/all_to_all | solution.py:99
  115.1 18.9 %all-to-all-done.3 = bf16[4,256,256]{2,0,1:T(4,128)(2,1)S(1)} async-done(((bf16[4,256,256]{2,0,1:T(4,128)(2,1)}), bf16[4,256,256]{2,0,1:T(4,128)(2,1)S(1)}, u32[]{:S(2)}, u32[]{:S(2)}) %all-to-all-start.3) | async-done | bytes 524320 | tf_op jit(solution)/shard_map/all_to_all | solution.py:99
  135.0 1.6 multiply_reduce_fusion
  136.6 1.8 multiply_convert_fusion.1
  139.3 1.8 copy-done.1
  141.0 1.7 convert.21
  143.5 2.1 slice_bitcast_fusion
  145.6 73.0 %while.21 = (s32[]{:T(128)}, f32[8,2,512,32]{2,3,0,1:T(8,128)}, bf16[8,2,512,32]{2,3,0,1:T(8,128)(2,1)S(1)}, bf16[8,2,512,32]{2,3,0,1:T(8,128)(2,1)}, bf16[8,2,512,32]{2,3,0,1:T(8,128)(2,1)S(1)}, /*index=5*/s32[]{:T(128)}) while((s32[]{:T(128)}, f32[8,2,512,32]{2,3,0,1:T(8,128)}, bf16[8,2,512,32]{2,3,0,1:T(8,128)(2,1)S(1)}, ...), condition=%wide.region_13.14_spmd, body=%wide.region_10.13_spmd.sunk | while | flops 67108864 | bytes 1507417 | solution.py:61
  149.1 3.8 %dot_general.47 = f32[2,512,32]{2,1,0:T(8,128)} custom-call(bf16[2,512,32]{2,1,0:T(8,128)(2,1)} %bitcast.178, bf16[2,512,32]{2,1,0:T(8,128)(2,1)} %bitcast.177, bf16[2,512,32]{2,1,0:T(8,128)(2,1)} %bitcast.179), custom_call_target="tpu_custom_call" | custom-call | flops 67108864 | bytes 196608 | tf_op jit(solution)/shard_map/while/body/eval_jaxpr/bij,bjd->bid/dot_general | solution.py:59
  158.2 3.8 %dot_general.47 = f32[2,512,32]{2,1,0:T(8,128)} custom-call(bf16[2,512,32]{2,1,0:T(8,128)(2,1)} %bitcast.178, bf16[2,512,32]{2,1,0:T(8,128)(2,1)} %bitcast.177, bf16[2,512,32]{2,1,0:T(8,128)(2,1)} %bitcast.179), custom_call_target="tpu_custom_call" | custom-call | flops 67108864 | bytes 196608 | tf_op jit(solution)/shard_map/while/body/eval_jaxpr/bij,bjd->bid/dot_general | solution.py:59
  167.3 3.8 %dot_general.47 = f32[2,512,32]{2,1,0:T(8,128)} custom-call(bf16[2,512,32]{2,1,0:T(8,128)(2,1)} %bitcast.178, bf16[2,512,32]{2,1,0:T(8,128)(2,1)} %bitcast.177, bf16[2,512,32]{2,1,0:T(8,128)(2,1)} %bitcast.179), custom_call_target="tpu_custom_call" | custom-call | flops 67108864 | bytes 196608 | tf_op jit(solution)/shard_map/while/body/eval_jaxpr/bij,bjd->bid/dot_general | solution.py:59
  176.4 3.8 %dot_general.47 = f32[2,512,32]{2,1,0:T(8,128)} custom-call(bf16[2,512,32]{2,1,0:T(8,128)(2,1)} %bitcast.178, bf16[2,512,32]{2,1,0:T(8,128)(2,1)} %bitcast.177, bf16[2,512,32]{2,1,0:T(8,128)(2,1)} %bitcast.179), custom_call_target="tpu_custom_call" | custom-call | flops 67108864 | bytes 196608 | tf_op jit(solution)/shard_map/while/body/eval_jaxpr/bij,bjd->bid/dot_general | solution.py:59
  185.6 3.8 %dot_general.47 = f32[2,512,32]{2,1,0:T(8,128)} custom-call(bf16[2,512,32]{2,1,0:T(8,128)(2,1)} %bitcast.178, bf16[2,512,32]{2,1,0:T(8,128)(2,1)} %bitcast.177, bf16[2,512,32]{2,1,0:T(8,128)(2,1)} %bitcast.179), custom_call_target="tpu_custom_call" | custom-call | flops 67108864 | bytes 196608 | tf_op jit(solution)/shard_map/while/body/eval_jaxpr/bij,bjd->bid/dot_general | solution.py:59
  194.7 3.8 %dot_general.47 = f32[2,512,32]{2,1,0:T(8,128)} custom-call(bf16[2,512,32]{2,1,0:T(8,128)(2,1)} %bitcast.178, bf16[2,512,32]{2,1,0:T(8,128)(2,1)} %bitcast.177, bf16[2,512,32]{2,1,0:T(8,128)(2,1)} %bitcast.179), custom_call_target="tpu_custom_call" | custom-call | flops 67108864 | bytes 196608 | tf_op jit(solution)/shard_map/while/body/eval_jaxpr/bij,bjd->bid/dot_general | solution.py:59
  203.8 3.8 %dot_general.47 = f32[2,512,32]{2,1,0:T(8,128)} custom-call(bf16[2,512,32]{2,1,0:T(8,128)(2,1)} %bitcast.178, bf16[2,512,32]{2,1,0:T(8,128)(2,1)} %bitcast.177, bf16[2,512,32]{2,1,0:T(8,128)(2,1)} %bitcast.179), custom_call_target="tpu_custom_call" | custom-call | flops 67108864 | bytes 196608 | tf_op jit(solution)/shard_map/while/body/eval_jaxpr/bij,bjd->bid/dot_general | solution.py:59
  212.9 3.8 %dot_general.47 = f32[2,512,32]{2,1,0:T(8,128)} custom-call(bf16[2,512,32]{2,1,0:T(8,128)(2,1)} %bitcast.178, bf16[2,512,32]{2,1,0:T(8,128)(2,1)} %bitcast.177, bf16[2,512,32]{2,1,0:T(8,128)(2,1)} %bitcast.179), custom_call_target="tpu_custom_call" | custom-call | flops 67108864 | bytes 196608 | tf_op jit(solution)/shard_map/while/body/eval_jaxpr/bij,bjd->bid/dot_general | solution.py:59
  218.6 1.8 fusion.55
  223.1 84.4 %all-gather.2.cloned.1.call-done = bf16[512,256,32]{0,2,1:T(8,128)(2,1)} async-done(((bf16[512,2,32]{0,2,1:T(8,128)(2,1)}), bf16[512,256,32]{0,2,1:T(8,128)(2,1)}) %all-gather.2.cloned.1.call-update) | async-done | bytes 8388624 | tf_op jit(solution)/shard_map/all_gather | solution.py:118
  307.6 9.4 %fusion.26 = bf16[2,256,32,32]{2,3,0,1:T(8,128)(2,1)} fusion(bf16[512,256,32]{0,2,1:T(8,128)(2,1)} %all-gather.2.cloned.1.call-done, bf16[512,2,64]{0,2,1:T(8,128)(2,1)S(1)} %convolution_convert_fusion), kind=kOutput, calls=%fused_computation.30 | convolution fusion | flops 537919488 | bytes 9502720 | tf_op jit(solution)/shard_map/sic,sjd->ijcd/dot_general | solution.py:119
  317.0 6.2 %copy.93 = bf16[2,256,32,32]{1,3,2,0:T(8,128)(2,1)S(1)} copy(bf16[2,256,32,32]{2,3,0,1:T(8,128)(2,1)} %fusion.26) | data formatting | bytes 2097152 | tf_op jit(solution)/shard_map/convert_element_type | solution.py:120
  (126 shorter events, 69.3 us)
Async XLA Ops:
  7.2 33.0 %copy-start = (bf16[256,1024]{1,0:T(8,128)(2,1)S(1)}, bf16[256,1024]{1,0:T(8,128)(2,1)}, u32[]{:S(2)}) copy-start(bf16[256,1024]{1,0:T(8,128)(2,1)} %param.18) | copy-start | bytes 1572868
  11.3 15.1 %all-to-all-start = ((bf16[8,1,8,2,256]{4,2,3,1,0:T(8,128)(2,1)}), bf16[8,1,8,2,256]{4,2,3,1,0:T(8,128)(2,1)S(1)}, u32[]{:S(2)}, u32[]{:S(2)}) async-start(bf16[8,1,8,2,256]{4,2,3,1,0:T(8,128)(2,1)} %stack.9), calls=%async_computation | async-start | bytes 131072 | tf_op jit(solution)/shard_map/all_to_all | solution.py:24
  27.2 25.2 %all-to-all-start.1 = ((bf16[8,8,8,2,256]{4,2,3,1,0:T(8,128)(2,1)}), bf16[8,8,8,2,256]{4,2,3,1,0:T(8,128)(2,1)S(1)}, u32[]{:S(2)}, u32[]{:S(2)}) async-start(bf16[8,8,8,2,256]{4,2,3,1,0:T(8,128)(2,1)} %stack.10), calls=%async_computation.1 | async-start | bytes 1048576 | tf_op jit(solution)/shard_map/all_to_all | solution.py:24
  44.2 2.6 copy-start.5
  65.6 37.8 %copy-start.2 = (bf16[4,256,256]{2,1,0:T(8,128)(2,1)S(1)}, bf16[4,256,256]{2,1,0:T(8,128)(2,1)}, u32[]{:S(2)}) copy-start(bf16[4,256,256]{2,1,0:T(8,128)(2,1)} %param.14) | copy-start | bytes 1572868
  65.6 37.8 %copy-start.8 = (bf16[256,256]{1,0:T(8,128)(2,1)S(1)}, bf16[256,256]{1,0:T(8,128)(2,1)}, u32[]{:S(2)}) copy-start(bf16[256,256]{1,0:T(8,128)(2,1)} %param.19) | copy-start | bytes 393220
  105.9 32.4 %copy-start.4 = (bf16[256,1024]{1,0:T(8,128)(2,1)S(1)}, bf16[256,1024]{1,0:T(8,128)(2,1)}, u32[]{:S(2)}) copy-start(bf16[256,1024]{1,0:T(8,128)(2,1)} %param.20) | copy-start | bytes 1572868
  105.9 28.0 %all-to-all-start.3 = ((bf16[4,256,256]{2,0,1:T(4,128)(2,1)}), bf16[4,256,256]{2,0,1:T(4,128)(2,1)S(1)}, u32[]{:S(2)}, u32[]{:S(2)}) async-start(bf16[4,256,256]{2,0,1:T(4,128)(2,1)} %copy.81), calls=%async_computation.3 | async-start | bytes 1048576 | tf_op jit(solution)/shard_map/all_to_all | solution.py:99
  114.8 192.8 %all-gather.2.cloned.1.call-start = ((), (), s32[]{:S(2)}) async-start(), calls=%async_computation.4 | async-start | bytes 8454144 | tf_op jit(solution)/shard_map/all_gather | solution.py:118
  139.1 1.9 copy-start.1
  145.6 74.9 %copy-start.7 = (bf16[256,256]{1,0:T(8,128)(2,1)S(1)}, bf16[256,256]{1,0:T(8,128)(2,1)}, u32[]{:S(2)}) copy-start(bf16[256,256]{1,0:T(8,128)(2,1)} %param.21) | copy-start | bytes 393220
  218.6 2.4 copy-start.9
  317.0 6.2 %copy-start.3 = (bf16[2,256,128]{2,1,0:T(8,128)(2,1)S(1)}, bf16[2,256,128]{2,1,0:T(8,128)(2,1)}, u32[]{:S(2)}) copy-start(bf16[2,256,128]{2,1,0:T(8,128)(2,1)} %param.15) | copy-start | bytes 393220
  317.0 6.2 %copy-start.6 = (bf16[1024,128]{1,0:T(8,128)(2,1)S(1)}, bf16[1024,128]{1,0:T(8,128)(2,1)}, u32[]{:S(2)}) copy-start(bf16[1024,128]{1,0:T(8,128)(2,1)} %param.23) | copy-start | bytes 786436
Sparse Core Ops, SparseCore 0:
  222.1 85.3 all-gather.1
